TPU v7x, 32 devices: a whole 2x2x4 slice. The times are simulated.
32 devices in a mesh: groups: 2 (over x), sph: 16 (over z, y, core).
Axes of the slice: x: 2, y: 2, z: 4, core: 2. Of those that a mesh axis runs over, the one named last changes fastest.
Arguments:
- positions: float32 [512, 3], P('sph'), may hold values from -8 to 8
- wave_vectors: float32 [256, 3], replicated, may hold values from -5 to 5
- pattern: float32 [2, 448, 256], replicated, may hold values from -6 to 6
- dir_index: int32 [64], P('groups'), parts along dimension 0, may hold values from 0 to 255
- mie: float32 [2, 448, 512], P(None, None, 'sph'), may hold values from -0.9 to 0.9
- trans_table: bfloat16 [8, 2, 448, 448], replicated, may hold values from -0.1875 to 0.1875
- pair_route: int32 [1024, 1], P('sph'), may hold values from 0 to 15; in each aligned block of 64 rows (0 to 63, 64 to 127, ...) at most 8 rows name the same one
- pair_source: int32 [1024], P('sph'), may hold values from 0 to 15
- pair_target: int32 [1024], P('sph'), may hold values from 0 to 15
- pair_class: int32 [1024], P('sph'), may hold values from 0 to 7
Outputs:
- scattered: bfloat16 [896, 32768], P(None, ('groups', 'sph')), parts along dimension 1
- extinction: float32 [64], P('groups'), parts along dimension 0
There are 2 independent parts, one for each index of `groups`. A program takes and returns all parts, laid end to end along the dimension named above; an argument that names none is the same for every part. Nothing has to cross between parts.
Inputs may be any that keep to these rules, and one draw needn't show every extreme that they name: `pair_route`: among the rows of one device no device is named by more than 8 pairs, and in every draw some device is named by exactly 8 of them.
All inputs are finite; a program needn't handle non-finite values.
Results may differ from a plain program's by a relative error of at most 0.0051.
Values may be sent and summed in bfloat16 or wider, within the bound.
No kernel may reach another device: no remote copies, remote signals or barrier semaphores. Data moves between devices by JAX's collectives and lax.ppermute only.
A program may use at most 192 MiB of HBM per device.

v0:
```python
import jax
import jax.numpy as jnp
from jax import lax
from jax.sharding import PartitionSpec as P

BLOCK = 2
HIGHEST_PRECISION = lax.Precision.HIGHEST


def incident_field(positions, wave_vectors, pattern, dir_index):
    table_rows = wave_vectors.shape[0]
    select = (jnp.arange(table_rows, dtype=jnp.int32)[:, None] == dir_index[None, :]).astype(
        jnp.float32
    )
    directions = jnp.dot(select.T, wave_vectors, precision=HIGHEST_PRECISION)
    phases = (
        positions[:, 0:1] * directions[None, :, 0]
        + positions[:, 1:2] * directions[None, :, 1]
        + positions[:, 2:3] * directions[None, :, 2]
    )
    cosine = jnp.cos(phases)
    sine_part = jnp.sin(phases)
    chosen = jnp.einsum("cmt,td->cmd", pattern, select, precision=HIGHEST_PRECISION)
    inc_real = cosine[None] * chosen[0][:, None, :] - sine_part[None] * chosen[1][:, None, :]
    inc_imag = cosine[None] * chosen[1][:, None, :] + sine_part[None] * chosen[0][:, None, :]
    return (inc_real, inc_imag)


def translate(trans_table, classes, block_values):
    item_count = classes.shape[0]
    mode_count = trans_table.shape[2]
    grouped_classes = classes.reshape(item_count // 8, 8)
    grouped_values = block_values.reshape((item_count // 8, 8) + block_values.shape[1:])

    def one_group(group_items):
        picked, values = group_items
        tables = trans_table[picked]
        data_real = values[:, :mode_count]
        data_imag = values[:, mode_count:]
        part_real = jnp.einsum(
            "kij,kjc->kic", tables[:, 0], data_real, preferred_element_type=jnp.float32
        ) - jnp.einsum("kij,kjc->kic", tables[:, 1], data_imag, preferred_element_type=jnp.float32)
        part_imag = jnp.einsum(
            "kij,kjc->kic", tables[:, 1], data_real, preferred_element_type=jnp.float32
        ) + jnp.einsum("kij,kjc->kic", tables[:, 0], data_imag, preferred_element_type=jnp.float32)
        return jnp.concatenate([part_real, part_imag], 1).astype(jnp.bfloat16)

    return lax.map(one_group, (grouped_classes, grouped_values)).reshape(block_values.shape)


def shards(
    positions,
    wave_vectors,
    pattern,
    dir_index,
    mie,
    trans_table,
    pair_route,
    pair_source,
    pair_target,
    pair_class,
):
    mode_count = pattern.shape[1]
    spheres = positions.shape[0]
    directions = dir_index.shape[0]
    columns = BLOCK * directions
    block_count = spheres // BLOCK
    devices = lax.axis_size("sph")
    pair_count = pair_source.shape[0]
    capacity = max(2, 2 * pair_count // devices)
    slot_count = devices * capacity
    inc_real, inc_imag = incident_field(positions, wave_vectors, pattern, dir_index)
    mie_real = mie[0][:, :, None]
    mie_imag = mie[1][:, :, None]
    scat_real = mie_real * inc_real - mie_imag * inc_imag
    scat_imag = mie_real * inc_imag + mie_imag * inc_real
    coeffs = jnp.concatenate([scat_real, scat_imag], 0).astype(jnp.bfloat16)
    block_data = coeffs.reshape(2 * mode_count, block_count, columns).transpose(1, 0, 2)
    dest_device = pair_route[:, 0]
    by_device = (dest_device[:, None] == jnp.arange(devices, dtype=jnp.int32)[None, :]).astype(
        jnp.int32
    )
    before = jnp.cumsum(by_device, axis=0) - by_device
    rank_in = jnp.sum(before * by_device, axis=1)
    slot_of = dest_device * capacity + rank_in
    slot_match = (jnp.arange(slot_count, dtype=jnp.int32)[:, None] == slot_of[None, :]).astype(
        jnp.int32
    )
    filled = jnp.sum(slot_match, axis=1)
    slot_pair = jnp.sum(slot_match * jnp.arange(pair_count, dtype=jnp.int32)[None, :], axis=1)
    slot_target = jnp.where(filled > 0, pair_target[slot_pair], -1)
    keep_slot = filled.astype(jnp.bfloat16)[:, None, None]
    computed = translate(trans_table, pair_class, block_data[pair_source])
    outgoing = computed[slot_pair] * keep_slot
    outgoing = outgoing.reshape(devices, capacity, 2 * mode_count, columns)
    arrived = lax.all_to_all(outgoing, "sph", split_axis=0, concat_axis=0, tiled=True)
    targets = lax.all_to_all(
        slot_target.reshape(devices, capacity), "sph", split_axis=0, concat_axis=0, tiled=True
    ).reshape(slot_count)
    partial_value = arrived.reshape(slot_count, 2 * mode_count, columns)
    gather_matrix = (jnp.arange(block_count, dtype=jnp.int32)[:, None] == targets[None, :]).astype(
        jnp.bfloat16
    )
    summed = jnp.dot(
        gather_matrix,
        partial_value.reshape(slot_count, 2 * mode_count * columns),
        preferred_element_type=jnp.float32,
    )
    summed = (
        summed.reshape(block_count, 2 * mode_count, columns)
        .transpose(1, 0, 2)
        .reshape(2 * mode_count, spheres, directions)
    )
    total_real = inc_real + summed[:mode_count]
    total_imag = inc_imag + summed[mode_count:]
    out_real = mie_real * total_real - mie_imag * total_imag
    out_imag = mie_real * total_imag + mie_imag * total_real
    scattered = (
        jnp.concatenate([out_real, out_imag], 0)
        .reshape(2 * mode_count, spheres * directions)
        .astype(jnp.bfloat16)
    )
    local_ext = jnp.sum(inc_real * out_real + inc_imag * out_imag, axis=(0, 1))
    extinction = lax.psum(local_ext, "sph")
    return (scattered, extinction)


def solution(mesh):
    placed = (
        P("sph", None),
        P(),
        P(),
        P("groups"),
        P(None, None, "sph"),
        P(),
        P("sph", None),
        P("sph"),
        P("sph"),
        P("sph"),
    )
    return jax.shard_map(
        shards,
        mesh=mesh,
        in_specs=placed,
        out_specs=(P(None, ("groups", "sph")), P("groups")),
        check_vma=False,
    )
```

profile of v0, /device:TPU:0, one launch (start us, length us, event | category | flops | bytes accessed | tf_op | source)
XLA Modules:
  0.0 671.2 jit_solution(2450275542576880069)
XLA Ops:
  3.2 1.6 gather_fusion.1
  5.5 7.4 %all-to-all-start = ((s32[16,1,8]{2,1,0:T(1,128)}), s32[16,1,8]{2,1,0:T(1,128)S(1)}, u32[]{:S(2)}, u32[]{:S(2)}) async-start(s32[16,1,8]{2,1,0:T(1,128)} %bitcast.24), calls=%async_computation | async-start | bytes 16384 | tf_op jit(solution)/shard_map/all_to_all | solution.py:97
  16.3 1.2 convolution_bitcast_fusion
  21.9 4.3 gather_fusion.2
  26.3 134.5 %while.10 = (s32[]{:T(128)}, bf16[8,8,896,64]{2,3,1,0:T(8,128)(2,1)}, s32[8,8]{1,0:T(8,128)S(1)}, bf16[8,2,448,448]{3,2,1,0:T(8,128)(2,1)}, bf16[8,8,896,64]{2,3,1,0:T(8,128)(2,1)}, /*index=5*/s32[]{:T(128)}) while((s32[]{:T(128)}, bf16[8,8,896,64]{2,3,1,0:T(8,128)(2,1)}, s32[8,8]{1,0:T(8,128)S(1)}, bf16[8,2,448,448]{3,2,1,0:T(8,128)(2,1)}, ...), condition=%wide.region_5.6_spmd, body=%wide.region_4.5_spmd.sunk | while | flops 824837120 | bytes 63836904 | solution.py:48
  26.3 7.0 %gather_fusion = bf16[8,2,448,448]{3,2,1,0:T(8,128)(2,1)} fusion(bf16[8,2,448,448]{3,2,1,0:T(8,128)(2,1)} %get-tuple-element.133, s32[1024]{0:T(1024)S(1)} %pad_clamp_fusion.4), kind=kCustom, calls=%fused_computation.clone.1 | custom fusion | bytes 12845088 | tf_op jit(solution)/shard_map/while/body/eval_jaxpr/gather | solution.py:37
  33.3 1.4 dynamic-slice_bitcast_fusion.2
  34.7 3.5 fusion.68
  38.2 1.2 fusion.69
  41.8 1.3 maximum_dynamic-update-slice_fusion.2
  43.1 7.0 %gather_fusion = bf16[8,2,448,448]{3,2,1,0:T(8,128)(2,1)} fusion(bf16[8,2,448,448]{3,2,1,0:T(8,128)(2,1)} %get-tuple-element.133, s32[1024]{0:T(1024)S(1)} %pad_clamp_fusion.4), kind=kCustom, calls=%fused_computation.clone.1 | custom fusion | bytes 12845088 | tf_op jit(solution)/shard_map/while/body/eval_jaxpr/gather | solution.py:37
  50.1 1.4 dynamic-slice_bitcast_fusion.2
  51.5 3.5 fusion.68
  55.0 1.2 fusion.69
  56.2 1.2 fusion.66
  58.6 1.3 maximum_dynamic-update-slice_fusion.2
  59.9 7.0 %gather_fusion = bf16[8,2,448,448]{3,2,1,0:T(8,128)(2,1)} fusion(bf16[8,2,448,448]{3,2,1,0:T(8,128)(2,1)} %get-tuple-element.133, s32[1024]{0:T(1024)S(1)} %pad_clamp_fusion.4), kind=kCustom, calls=%fused_computation.clone.1 | custom fusion | bytes 12845088 | tf_op jit(solution)/shard_map/while/body/eval_jaxpr/gather | solution.py:37
  66.9 1.4 dynamic-slice_bitcast_fusion.2
  68.3 3.5 fusion.68
  71.8 1.2 fusion.69
  73.0 1.2 fusion.66
  75.4 1.3 maximum_dynamic-update-slice_fusion.2
  76.7 7.0 %gather_fusion = bf16[8,2,448,448]{3,2,1,0:T(8,128)(2,1)} fusion(bf16[8,2,448,448]{3,2,1,0:T(8,128)(2,1)} %get-tuple-element.133, s32[1024]{0:T(1024)S(1)} %pad_clamp_fusion.4), kind=kCustom, calls=%fused_computation.clone.1 | custom fusion | bytes 12845088 | tf_op jit(solution)/shard_map/while/body/eval_jaxpr/gather | solution.py:37
  83.7 1.4 dynamic-slice_bitcast_fusion.2
  85.1 3.5 fusion.68
  88.6 1.2 fusion.69
  89.8 1.2 fusion.66
  92.2 1.3 maximum_dynamic-update-slice_fusion.2
  93.5 7.0 %gather_fusion = bf16[8,2,448,448]{3,2,1,0:T(8,128)(2,1)} fusion(bf16[8,2,448,448]{3,2,1,0:T(8,128)(2,1)} %get-tuple-element.133, s32[1024]{0:T(1024)S(1)} %pad_clamp_fusion.4), kind=kCustom, calls=%fused_computation.clone.1 | custom fusion | bytes 12845088 | tf_op jit(solution)/shard_map/while/body/eval_jaxpr/gather | solution.py:37
  100.5 1.4 dynamic-slice_bitcast_fusion.2
  101.9 3.5 fusion.68
  105.4 1.2 fusion.69
  106.6 1.2 fusion.66
  109.0 1.3 maximum_dynamic-update-slice_fusion.2
  110.3 7.0 %gather_fusion = bf16[8,2,448,448]{3,2,1,0:T(8,128)(2,1)} fusion(bf16[8,2,448,448]{3,2,1,0:T(8,128)(2,1)} %get-tuple-element.133, s32[1024]{0:T(1024)S(1)} %pad_clamp_fusion.4), kind=kCustom, calls=%fused_computation.clone.1 | custom fusion | bytes 12845088 | tf_op jit(solution)/shard_map/while/body/eval_jaxpr/gather | solution.py:37
  117.3 1.4 dynamic-slice_bitcast_fusion.2
  118.7 3.5 fusion.68
  122.2 1.2 fusion.69
  123.4 1.2 fusion.66
  125.8 1.3 maximum_dynamic-update-slice_fusion.2
  127.1 7.0 %gather_fusion = bf16[8,2,448,448]{3,2,1,0:T(8,128)(2,1)} fusion(bf16[8,2,448,448]{3,2,1,0:T(8,128)(2,1)} %get-tuple-element.133, s32[1024]{0:T(1024)S(1)} %pad_clamp_fusion.4), kind=kCustom, calls=%fused_computation.clone.1 | custom fusion | bytes 12845088 | tf_op jit(solution)/shard_map/while/body/eval_jaxpr/gather | solution.py:37
  134.1 1.4 dynamic-slice_bitcast_fusion.2
  135.5 3.4 fusion.68
  139.0 1.2 fusion.69
  140.2 1.2 fusion.66
  142.6 1.3 maximum_dynamic-update-slice_fusion.2
  144.0 7.0 %gather_fusion = bf16[8,2,448,448]{3,2,1,0:T(8,128)(2,1)} fusion(bf16[8,2,448,448]{3,2,1,0:T(8,128)(2,1)} %get-tuple-element.133, s32[1024]{0:T(1024)S(1)} %pad_clamp_fusion.4), kind=kCustom, calls=%fused_computation.clone.1 | custom fusion | bytes 12845088 | tf_op jit(solution)/shard_map/while/body/eval_jaxpr/gather | solution.py:37
  151.0 1.4 dynamic-slice_bitcast_fusion.2
  152.4 3.5 fusion.68
  155.9 1.2 fusion.69
  157.1 1.2 fusion.66
  159.5 1.3 maximum_dynamic-update-slice_fusion.2
  160.7 12.3 %gather_fusion.3 = bf16[128,896,64]{1,2,0:T(8,128)(2,1)} fusion(bf16[64,896,64]{1,2,0:T(8,128)(2,1)} %bitcast.33, s32[1024]{0:T(1024)S(1)} %pad_clamp_fusion.2), kind=kCustom, calls=%fused_computation.3 | custom fusion | bytes 29360640 | tf_op jit(solution)/shard_map/gather | solution.py:94
  173.1 13.5 %broadcast_multiply_fusion = bf16[16,8,896,64]{2,3,1,0:T(8,128)(2,1)} fusion(bf16[16,8,896,64]{2,3,1,0:T(8,128)(2,1)} %bitcast.236, bf16[16,8]{1,0:T(8,128)(2,1)S(1)} %convert_element_type.32), kind=kLoop, calls=%fused_computation.29 | loop fusion | flops 7340032 | bytes 29360384 | tf_op jit(solution)/shard_map/mul | solution.py:94
  186.6 6.0 all-to-all-start.1
  194.7 258.1 %all-to-all-done.1 = bf16[16,8,896,64]{2,3,1,0:T(8,128)(2,1)} async-done(((bf16[16,8,896,64]{2,3,1,0:T(8,128)(2,1)}), bf16[16,8,896,64]{2,3,1,0:T(8,128)(2,1)}, u32[]{:S(2)}, u32[]{:S(2)}) %all-to-all-start.1) | async-done | bytes 14680096 | tf_op jit(solution)/shard_map/all_to_all | solution.py:96
  452.8 26.5 %copy.80 = bf16[16,8,896,64]{3,2,1,0:T(8,128)(2,1)} copy(bf16[16,8,896,64]{2,3,1,0:T(8,128)(2,1)} %all-to-all-done.1) | data formatting | bytes 29360128 | tf_op jit(solution)/shard_map/all_to_all | solution.py:96
  479.3 28.1 %reshape_reshape.3 = bf16[128,57344]{1,0:T(8,128)(2,1)} reshape(bf16[16,8,896,64]{3,2,1,0:T(8,128)(2,1)} %copy.80) | data formatting | bytes 29360128 | tf_op jit(solution)/shard_map/reshape;reshape | solution.py:106
  507.4 20.2 %copy.81 = bf16[57344,128]{1,0:T(8,128)(2,1)} copy(bf16[57344,128]{0,1:T(8,128)(2,1)} %bitcast.238) | data formatting | bytes 29360128 | tf_op jit(solution)/shard_map/dot_general | solution.py:104
  527.6 35.5 %fusion.34 = f32[896,16,64]{0,1,2:T(8,128)} fusion(bf16[896,64,128]{2,1,0:T(8,128)(2,1)} %bitcast.237, s32[128]{0:T(128)S(1)} %eq.64), kind=kOutput, calls=%fused_computation.61 | convolution fusion | flops 234883072 | bytes 18350592 | tf_op jit(solution)/shard_map/dot_general | solution.py:104
  563.1 9.9 %add_reduce_fusion = (f32[16,64]{0,1:T(8,128)S(1)}, f32[448,16,64]{0,1,2:T(8,128)S(1)}, f32[448,16,64]{0,1,2:T(8,128)S(1)}) fusion(f32[448,16,64]{0,2,1:T(8,128)S(1)} %bitcast.241, f32[448,16,64]{0,2,1:T(8,128)} %bitcast.247, f32[448,16,64]{0,2,1:T(8,128)S(1)} %bitcast.243, f32[448,16,64]{0,2,1:T(8,128)S(1)} %bitcast.245, f32[16,64]{0,1:T(8,128)S(1)} %copy.87, ...), kind=kLoop, calls=%fused_computation.60 | loop fusion | flops 8256512 | bytes 14692352 | tf_op jit(solution)/shard_map/reduce_sum | solution.py:123
  575.6 1.7 fusion.19
  577.8 2.4 copy.96
  580.4 90.4 %psum.7 = f32[32]{0:T(128)} all-reduce(f32[32]{0:T(128)S(1)} %reduce_sum.51), channel_id=1, replica_groups=mesh['groups'=2,'sph'=16] {'sph'}, use_global_device_ids=true, to_apply=%region_8.9 | all-reduce | flops 32 | bytes 256 | tf_op jit(solution)/shard_map/psum | solution.py:124
  (152 shorter events, 26.9 us)
Async XLA Ops:
  0.6 15.6 %copy-start = (f32[2,448,256]{2,1,0:T(8,128)S(1)}, f32[2,448,256]{2,1,0:T(8,128)}, u32[]{:S(2)}) copy-start(f32[2,448,256]{2,1,0:T(8,128)} %param.14) | copy-start | bytes 2752516
  0.6 16.9 %copy-start.20 = (s32[64]{0:T(128)S(1)}, s32[64]{0:T(128)}, u32[]{:S(2)}) copy-start(s32[64]{0:T(128)} %param.19) | copy-start | bytes 772
  0.7 16.9 %copy-start.19 = (s32[64]{0:T(128)S(1)}, s32[64]{0:T(128)}, u32[]{:S(2)}) copy-start(s32[64]{0:T(128)} %param.21) | copy-start | bytes 772
  0.7 17.0 %copy-start.18 = (f32[2,448,32]{1,2,0:T(8,128)S(1)}, f32[2,448,32]{1,2,0:T(8,128)}, u32[]{:S(2)}) copy-start(f32[2,448,32]{1,2,0:T(8,128)} %param.16) | copy-start | bytes 344068
  5.5 181.1 %all-to-all-start = ((s32[16,1,8]{2,1,0:T(1,128)}), s32[16,1,8]{2,1,0:T(1,128)S(1)}, u32[]{:S(2)}, u32[]{:S(2)}) async-start(s32[16,1,8]{2,1,0:T(1,128)} %bitcast.24), calls=%async_computation | async-start | bytes 16384 | tf_op jit(solution)/shard_map/all_to_all | solution.py:97
  17.7 0.6 copy-start.12
  17.7 0.6 copy-start.14
  17.7 0.6 copy-start.10
  17.7 0.9 copy-start.16
  18.0 1.3 copy-start.3
  18.3 1.7 copy-start.5
  18.6 2.5 copy-start.7
  18.9 2.5 copy-start.9
  33.3 4.9 copy-start.2
  50.1 4.9 copy-start.2
  66.9 4.9 copy-start.2
  83.7 4.9 copy-start.2
  100.5 4.9 copy-start.2
  117.3 4.9 copy-start.2
  134.1 4.9 copy-start.2
  151.0 4.9 copy-start.2
  186.6 266.2 %all-to-all-start.1 = ((bf16[16,8,896,64]{2,3,1,0:T(8,128)(2,1)}), bf16[16,8,896,64]{2,3,1,0:T(8,128)(2,1)}, u32[]{:S(2)}, u32[]{:S(2)}) async-start(bf16[16,8,896,64]{2,3,1,0:T(8,128)(2,1)} %broadcast_multiply_fusion), calls=%async_computation.1 | async-start | bytes 29360128 | tf_op jit(solution)/shard_map/all_to_all | solution.py:96
  527.6 35.5 %copy-start.4 = (f32[448,32,32]{0,2,1:T(8,128)S(1)}, f32[448,32,32]{0,2,1:T(8,128)}, u32[]{:S(2)}) copy-start(f32[448,32,32]{0,2,1:T(8,128)} %copy-done.3) | copy-start | bytes 5505028
  527.6 35.5 %copy-start.6 = (f32[448,32,32]{0,2,1:T(8,128)S(1)}, f32[448,32,32]{0,2,1:T(8,128)}, u32[]{:S(2)}) copy-start(f32[448,32,32]{0,2,1:T(8,128)} %copy-done.5) | copy-start | bytes 5505028
  527.6 35.5 %copy-start.8 = (f32[448,32,32]{0,2,1:T(8,128)S(1)}, f32[448,32,32]{0,2,1:T(8,128)}, u32[]{:S(2)}) copy-start(f32[448,32,32]{0,2,1:T(8,128)} %copy-done.7) | copy-start | bytes 5505028
  574.3 1.3 copy-start.11
  574.3 1.3 copy-start.13
  574.3 1.3 copy-start.15
  574.3 1.3 copy-start.17
  577.2 93.6 %copy-start.1 = (f32[2,448,256]{2,1,0:T(8,128)S(1)}, f32[2,448,256]{2,1,0:T(8,128)}, u32[]{:S(2)}) copy-start(f32[2,448,256]{2,1,0:T(8,128)} %param.14) | copy-start | bytes 2752516
where the time goes:
time: 683 us; the launch traced here: 671 us
  waiting for transfers between devices  258 us (38%)
  local copies, waits for them, and re-layouts  172 us (25%)
  matrix products  94.1 us (14%)
  blocking collectives  90.4 us (13%)
  other arithmetic  41 us (6%)
  starting transfers between devices  13.5 us (2%)
    all_to_all x1, waiting for transfers between devices, shards(): lax.all_to_all(outgoing, 'sph', split_axis=0, concat_axis=0, tiled=True)  258 us
    psum x1, blocking collectives, shards(): extinction = lax.psum(local_ext, 'sph')  90.4 us
    gather x8, local copies, waits for them, and re-layouts, one_group(): tables = trans_table[picked]  56.2 us
    dot_general x1, matrix products, shards(): jnp.dot(gather_matrix, partial_value.reshape(slot_count, 2 * mode_count *...  35.5 us
    another operation x1, local copies, waits for them, and re-layouts, shards(): partial_value.reshape(slot_count, 2 * mode_count * columns)  28.1 us
    dot_general x8, matrix products, one_group(): jnp.einsum('kij,kjc->kic', tables[:, 0], data_real, preferred_element_typ...  27.6 us
    all_to_all x1, local copies, waits for them, and re-layouts, shards(): lax.all_to_all(outgoing, 'sph', split_axis=0, concat_axis=0, tiled=True)  26.5 us
    dot_general x1, local copies, waits for them, and re-layouts, shards(): jnp.dot(gather_matrix, partial_value.reshape(slot_count, 2 * mode_count *...  20.2 us
  transfers between devices with their start and end apart: 2, of which 1 were waited for; matrix products, arithmetic and copies ran while one was open for 26% of the time, Pallas kernels for 0%

commit v1 on v0

--- a/solution.py
+++ b/solution.py
@@ -121,7 +121,13 @@
         .astype(jnp.bfloat16)
     )
     local_ext = jnp.sum(inc_real * out_real + inc_imag * out_imag, axis=(0, 1))
-    extinction = lax.psum(local_ext, "sph")
+    size = lax.axis_size("sph")
+    extinction, reach = (local_ext, 1)
+    while reach < size:
+        extinction = extinction + lax.ppermute(
+            extinction, "sph", [(i, i ^ reach) for i in range(size)]
+        )
+        reach = 2 * reach
     return (scattered, extinction)
 
 

time: 683 us -> 660 us (0.966)
  blocking collectives: 90.4 us -> 0 us
  starting transfers between devices: 13.5 us -> 77.6 us
    psum x1 -> x0, blocking collectives: 90.4 us -> none  [shards(): extinction = lax.psum(local_ext, 'sph')]
    ppermute x0 -> x4, starting transfers between devices: none -> 64.1 us  [shards(): lax.ppermute(extinction, 'sph', [(i, i ^ reach) for i in range(size)])]
  transfers between devices with their start and end apart: 2 -> 6, of which waited for: 1 -> 2; matrix products, arithmetic and copies ran while one was open for 26% -> 28% of each run, Pallas kernels for 0% -> 0%
where the time goes in v1:
time: 660 us; the launch traced here: 649 us
  waiting for transfers between devices  258 us (39%)
  local copies, waits for them, and re-layouts  174 us (26%)
  matrix products  94.1 us (14%)
  starting transfers between devices  77.6 us (12%)
  other arithmetic  42.9 us (6%)
    all_to_all x1, waiting for transfers between devices, shards(): lax.all_to_all(outgoing, 'sph', split_axis=0, concat_axis=0, tiled=True)  258 us
    ppermute x4, starting transfers between devices, shards(): lax.ppermute(extinction, 'sph', [(i, i ^ reach) for i in range(size)])  64.1 us
    gather x8, local copies, waits for them, and re-layouts, one_group(): tables = trans_table[picked]  56.1 us
    dot_general x1, matrix products, shards(): jnp.dot(gather_matrix, partial_value.reshape(slot_count, 2 * mode_count *...  35.5 us
    another operation x1, local copies, waits for them, and re-layouts, shards(): partial_value.reshape(slot_count, 2 * mode_count * columns)  28.1 us
    dot_general x8, matrix products, one_group(): jnp.einsum('kij,kjc->kic', tables[:, 0], data_real, preferred_element_typ...  27.6 us
    all_to_all x1, local copies, waits for them, and re-layouts, shards(): lax.all_to_all(outgoing, 'sph', split_axis=0, concat_axis=0, tiled=True)  26.5 us
    dot_general x1, local copies, waits for them, and re-layouts, shards(): jnp.dot(gather_matrix, partial_value.reshape(slot_count, 2 * mode_count *...  20.1 us
  transfers between devices with their start and end apart: 6, of which 2 were waited for; matrix products, arithmetic and copies ran while one was open for 28% of the time, Pallas kernels for 0%

profile of v1, /device:TPU:0, one launch (start us, length us, event | category | flops | bytes accessed | tf_op | source)
XLA Modules:
  0.0 648.7 jit_solution(17065103738715006862)
XLA Ops:
  3.2 1.6 gather_fusion.1
  5.5 7.4 %all-to-all-start = ((s32[16,1,8]{2,1,0:T(1,128)}), s32[16,1,8]{2,1,0:T(1,128)S(1)}, u32[]{:S(2)}, u32[]{:S(2)}) async-start(s32[16,1,8]{2,1,0:T(1,128)} %bitcast.24), calls=%async_computation | async-start | bytes 16384 | tf_op jit(solution)/shard_map/all_to_all | solution.py:97
  16.3 1.2 convolution_bitcast_fusion
  21.9 4.3 gather_fusion.2
  26.2 134.4 %while.10 = (s32[]{:T(128)}, bf16[8,8,896,64]{2,3,1,0:T(8,128)(2,1)}, s32[8,8]{1,0:T(8,128)S(1)}, bf16[8,2,448,448]{3,2,1,0:T(8,128)(2,1)}, bf16[8,8,896,64]{2,3,1,0:T(8,128)(2,1)}, /*index=5*/s32[]{:T(128)}) while((s32[]{:T(128)}, bf16[8,8,896,64]{2,3,1,0:T(8,128)(2,1)}, s32[8,8]{1,0:T(8,128)S(1)}, bf16[8,2,448,448]{3,2,1,0:T(8,128)(2,1)}, ...), condition=%wide.region_5.6_spmd, body=%wide.region_4.5_spmd.sunk | while | flops 824837120 | bytes 63836904 | solution.py:48
  26.3 7.0 %gather_fusion = bf16[8,2,448,448]{3,2,1,0:T(8,128)(2,1)} fusion(bf16[8,2,448,448]{3,2,1,0:T(8,128)(2,1)} %get-tuple-element.133, s32[1024]{0:T(1024)S(1)} %pad_clamp_fusion.4), kind=kCustom, calls=%fused_computation.clone.1 | custom fusion | bytes 12845088 | tf_op jit(solution)/shard_map/while/body/eval_jaxpr/gather | solution.py:37
  33.3 1.4 dynamic-slice_bitcast_fusion.2
  34.7 3.5 fusion.68
  38.1 1.2 fusion.69
  41.8 1.3 maximum_dynamic-update-slice_fusion.2
  43.1 7.0 %gather_fusion = bf16[8,2,448,448]{3,2,1,0:T(8,128)(2,1)} fusion(bf16[8,2,448,448]{3,2,1,0:T(8,128)(2,1)} %get-tuple-element.133, s32[1024]{0:T(1024)S(1)} %pad_clamp_fusion.4), kind=kCustom, calls=%fused_computation.clone.1 | custom fusion | bytes 12845088 | tf_op jit(solution)/shard_map/while/body/eval_jaxpr/gather | solution.py:37
  50.1 1.4 dynamic-slice_bitcast_fusion.2
  51.5 3.5 fusion.68
  55.0 1.2 fusion.69
  56.2 1.2 fusion.66
  58.6 1.3 maximum_dynamic-update-slice_fusion.2
  59.9 7.0 %gather_fusion = bf16[8,2,448,448]{3,2,1,0:T(8,128)(2,1)} fusion(bf16[8,2,448,448]{3,2,1,0:T(8,128)(2,1)} %get-tuple-element.133, s32[1024]{0:T(1024)S(1)} %pad_clamp_fusion.4), kind=kCustom, calls=%fused_computation.clone.1 | custom fusion | bytes 12845088 | tf_op jit(solution)/shard_map/while/body/eval_jaxpr/gather | solution.py:37
  67.0 1.4 dynamic-slice_bitcast_fusion.2
  68.4 3.5 fusion.68
  71.8 1.2 fusion.69
  75.4 1.2 maximum_dynamic-update-slice_fusion.2
  76.7 7.0 %gather_fusion = bf16[8,2,448,448]{3,2,1,0:T(8,128)(2,1)} fusion(bf16[8,2,448,448]{3,2,1,0:T(8,128)(2,1)} %get-tuple-element.133, s32[1024]{0:T(1024)S(1)} %pad_clamp_fusion.4), kind=kCustom, calls=%fused_computation.clone.1 | custom fusion | bytes 12845088 | tf_op jit(solution)/shard_map/while/body/eval_jaxpr/gather | solution.py:37
  83.7 1.4 dynamic-slice_bitcast_fusion.2
  85.1 3.5 fusion.68
  88.6 1.2 fusion.69
  92.2 1.3 maximum_dynamic-update-slice_fusion.2
  93.5 7.0 %gather_fusion = bf16[8,2,448,448]{3,2,1,0:T(8,128)(2,1)} fusion(bf16[8,2,448,448]{3,2,1,0:T(8,128)(2,1)} %get-tuple-element.133, s32[1024]{0:T(1024)S(1)} %pad_clamp_fusion.4), kind=kCustom, calls=%fused_computation.clone.1 | custom fusion | bytes 12845088 | tf_op jit(solution)/shard_map/while/body/eval_jaxpr/gather | solution.py:37
  100.5 1.4 dynamic-slice_bitcast_fusion.2
  101.9 3.5 fusion.68
  105.4 1.2 fusion.69
  106.6 1.2 fusion.66
  109.0 1.2 maximum_dynamic-update-slice_fusion.2
  110.3 7.0 %gather_fusion = bf16[8,2,448,448]{3,2,1,0:T(8,128)(2,1)} fusion(bf16[8,2,448,448]{3,2,1,0:T(8,128)(2,1)} %get-tuple-element.133, s32[1024]{0:T(1024)S(1)} %pad_clamp_fusion.4), kind=kCustom, calls=%fused_computation.clone.1 | custom fusion | bytes 12845088 | tf_op jit(solution)/shard_map/while/body/eval_jaxpr/gather | solution.py:37
  117.3 1.4 dynamic-slice_bitcast_fusion.2
  118.7 3.5 fusion.68
  122.2 1.2 fusion.69
  123.4 1.2 fusion.66
  125.8 1.3 maximum_dynamic-update-slice_fusion.2
  127.1 7.0 %gather_fusion = bf16[8,2,448,448]{3,2,1,0:T(8,128)(2,1)} fusion(bf16[8,2,448,448]{3,2,1,0:T(8,128)(2,1)} %get-tuple-element.133, s32[1024]{0:T(1024)S(1)} %pad_clamp_fusion.4), kind=kCustom, calls=%fused_computation.clone.1 | custom fusion | bytes 12845088 | tf_op jit(solution)/shard_map/while/body/eval_jaxpr/gather | solution.py:37
  134.1 1.4 dynamic-slice_bitcast_fusion.2
  135.5 3.5 fusion.68
  138.9 1.2 fusion.69
  140.2 1.2 fusion.66
  142.6 1.3 maximum_dynamic-update-slice_fusion.2
  143.9 7.0 %gather_fusion = bf16[8,2,448,448]{3,2,1,0:T(8,128)(2,1)} fusion(bf16[8,2,448,448]{3,2,1,0:T(8,128)(2,1)} %get-tuple-element.133, s32[1024]{0:T(1024)S(1)} %pad_clamp_fusion.4), kind=kCustom, calls=%fused_computation.clone.1 | custom fusion | bytes 12845088 | tf_op jit(solution)/shard_map/while/body/eval_jaxpr/gather | solution.py:37
  150.9 1.4 dynamic-slice_bitcast_fusion.2
  152.3 3.4 fusion.68
  155.8 1.2 fusion.69
  159.4 1.3 maximum_dynamic-update-slice_fusion.2
  160.7 12.3 %gather_fusion.3 = bf16[128,896,64]{1,2,0:T(8,128)(2,1)} fusion(bf16[64,896,64]{1,2,0:T(8,128)(2,1)} %bitcast.33, s32[1024]{0:T(1024)S(1)} %pad_clamp_fusion.2), kind=kCustom, calls=%fused_computation.3 | custom fusion | bytes 29360640 | tf_op jit(solution)/shard_map/gather | solution.py:94
  173.0 13.4 %broadcast_multiply_fusion = bf16[16,8,896,64]{2,3,1,0:T(8,128)(2,1)} fusion(bf16[16,8,896,64]{2,3,1,0:T(8,128)(2,1)} %bitcast.236, bf16[16,8]{1,0:T(8,128)(2,1)S(1)} %convert_element_type.32), kind=kLoop, calls=%fused_computation.29 | loop fusion | flops 7340032 | bytes 29360384 | tf_op jit(solution)/shard_map/mul | solution.py:94
  186.4 6.0 all-to-all-start.1
  194.5 258.1 %all-to-all-done.1 = bf16[16,8,896,64]{2,3,1,0:T(8,128)(2,1)} async-done(((bf16[16,8,896,64]{2,3,1,0:T(8,128)(2,1)}), bf16[16,8,896,64]{2,3,1,0:T(8,128)(2,1)}, u32[]{:S(2)}, u32[]{:S(2)}) %all-to-all-start.1) | async-done | bytes 14680096 | tf_op jit(solution)/shard_map/all_to_all | solution.py:96
  452.6 26.5 %copy.80 = bf16[16,8,896,64]{3,2,1,0:T(8,128)(2,1)} copy(bf16[16,8,896,64]{2,3,1,0:T(8,128)(2,1)} %all-to-all-done.1) | data formatting | bytes 29360128 | tf_op jit(solution)/shard_map/all_to_all | solution.py:96
  479.1 28.1 %reshape_reshape.3 = bf16[128,57344]{1,0:T(8,128)(2,1)} reshape(bf16[16,8,896,64]{3,2,1,0:T(8,128)(2,1)} %copy.80) | data formatting | bytes 29360128 | tf_op jit(solution)/shard_map/reshape;reshape | solution.py:106
  507.2 20.1 %copy.81 = bf16[57344,128]{1,0:T(8,128)(2,1)} copy(bf16[57344,128]{0,1:T(8,128)(2,1)} %bitcast.238) | data formatting | bytes 29360128 | tf_op jit(solution)/shard_map/dot_general | solution.py:104
  527.4 35.5 %fusion.34 = f32[896,16,64]{0,1,2:T(8,128)} fusion(bf16[896,64,128]{2,1,0:T(8,128)(2,1)} %bitcast.237, s32[128]{0:T(128)S(1)} %eq.64), kind=kOutput, calls=%fused_computation.61 | convolution fusion | flops 234883072 | bytes 18350592 | tf_op jit(solution)/shard_map/dot_general | solution.py:104
  562.9 11.4 %add_reduce_fusion = (f32[16,64]{0,1:T(8,128)S(1)}, f32[448,16,64]{0,1,2:T(8,128)}, f32[448,16,64]{0,1,2:T(8,128)}) fusion(f32[448,16,64]{0,2,1:T(8,128)S(1)} %bitcast.241, f32[448,16,64]{0,2,1:T(8,128)} %bitcast.247, f32[448,16,64]{0,2,1:T(8,128)S(1)} %bitcast.243, f32[448,16,64]{0,2,1:T(8,128)S(1)} %bitcast.245, f32[16,64]{0,1:T(8,128)S(1)} %copy.87, ...), kind=kLoop, calls=%fused_computation.60 | loop fusion | flops 8256512 | bytes 14692352 | tf_op jit(solution)/shard_map/reduce_sum | solution.py:123
  575.4 3.0 copy.83
  578.4 20.3 %collective-permute-start.1 = (f32[32]{0:T(128)S(1)}, f32[32]{0:T(128)S(1)}, u32[]{:S(2)}, u32[]{:S(2)}) collective-permute-start(f32[32]{0:T(128)S(1)} %add.156), channel_id=1, source_target_pairs={{0,2},{1,3},{2,0},{3,1},{4,6},{5,7},{6,4},{7,5},{8,10},{9,11},{10,... | collective-permute-start | bytes 392 | tf_op jit(solution)/shard_map/ppermute | solution.py:127
  600.3 39.3 %collective-permute-start.2 = (f32[32]{0:T(128)S(1)}, f32[32]{0:T(128)S(1)}, u32[]{:S(2)}, u32[]{:S(2)}) collective-permute-start(f32[32]{0:T(128)S(1)} %add.157), channel_id=1, source_target_pairs={{0,4},{1,5},{2,6},{3,7},{4,0},{5,1},{6,2},{7,3},{8,12},{9,13},{10,... | collective-permute-start | bytes 392 | tf_op jit(solution)/shard_map/ppermute | solution.py:127
  639.6 1.6 fusion.19
  641.2 3.5 collective-permute-start.3
  645.3 2.4 copy.96
  (165 shorter events, 31.2 us)
Async XLA Ops:
  0.6 15.6 %copy-start = (f32[2,448,256]{2,1,0:T(8,128)S(1)}, f32[2,448,256]{2,1,0:T(8,128)}, u32[]{:S(2)}) copy-start(f32[2,448,256]{2,1,0:T(8,128)} %param.14) | copy-start | bytes 2752516
  0.6 16.9 %copy-start.21 = (s32[64]{0:T(128)S(1)}, s32[64]{0:T(128)}, u32[]{:S(2)}) copy-start(s32[64]{0:T(128)} %param.19) | copy-start | bytes 772
  0.7 16.9 %copy-start.20 = (s32[64]{0:T(128)S(1)}, s32[64]{0:T(128)}, u32[]{:S(2)}) copy-start(s32[64]{0:T(128)} %param.21) | copy-start | bytes 772
  0.7 17.0 %copy-start.19 = (f32[2,448,32]{1,2,0:T(8,128)S(1)}, f32[2,448,32]{1,2,0:T(8,128)}, u32[]{:S(2)}) copy-start(f32[2,448,32]{1,2,0:T(8,128)} %param.16) | copy-start | bytes 344068
  5.5 180.9 %all-to-all-start = ((s32[16,1,8]{2,1,0:T(1,128)}), s32[16,1,8]{2,1,0:T(1,128)S(1)}, u32[]{:S(2)}, u32[]{:S(2)}) async-start(s32[16,1,8]{2,1,0:T(1,128)} %bitcast.24), calls=%async_computation | async-start | bytes 16384 | tf_op jit(solution)/shard_map/all_to_all | solution.py:97
  17.6 0.6 copy-start.13
  17.7 0.6 copy-start.15
  17.7 0.6 copy-start.11
  17.7 0.9 copy-start.17
  18.0 1.4 copy-start.3
  18.3 1.7 copy-start.5
  18.6 2.5 copy-start.7
  18.8 2.4 copy-start.9
  33.3 4.9 copy-start.2
  50.1 4.9 copy-start.2
  67.0 4.9 copy-start.2
  83.7 4.9 copy-start.2
  100.5 4.9 copy-start.2
  117.3 4.9 copy-start.2
  134.1 4.9 copy-start.2
  150.9 4.9 copy-start.2
  186.4 266.2 %all-to-all-start.1 = ((bf16[16,8,896,64]{2,3,1,0:T(8,128)(2,1)}), bf16[16,8,896,64]{2,3,1,0:T(8,128)(2,1)}, u32[]{:S(2)}, u32[]{:S(2)}) async-start(bf16[16,8,896,64]{2,3,1,0:T(8,128)(2,1)} %broadcast_multiply_fusion), calls=%async_computation.1 | async-start | bytes 29360128 | tf_op jit(solution)/shard_map/all_to_all | solution.py:96
  527.4 35.5 %copy-start.4 = (f32[448,32,32]{0,2,1:T(8,128)S(1)}, f32[448,32,32]{0,2,1:T(8,128)}, u32[]{:S(2)}) copy-start(f32[448,32,32]{0,2,1:T(8,128)} %copy-done.3) | copy-start | bytes 5505028
  527.4 35.5 %copy-start.6 = (f32[448,32,32]{0,2,1:T(8,128)S(1)}, f32[448,32,32]{0,2,1:T(8,128)}, u32[]{:S(2)}) copy-start(f32[448,32,32]{0,2,1:T(8,128)} %copy-done.5) | copy-start | bytes 5505028
  527.4 35.5 %copy-start.8 = (f32[448,32,32]{0,2,1:T(8,128)S(1)}, f32[448,32,32]{0,2,1:T(8,128)}, u32[]{:S(2)}) copy-start(f32[448,32,32]{0,2,1:T(8,128)} %copy-done.7) | copy-start | bytes 5505028
  574.4 4.0 collective-permute-start
  575.4 23.3 %copy-start.10 = (f32[448,16,64]{0,1,2:T(8,128)S(1)}, f32[448,16,64]{0,1,2:T(8,128)}, u32[]{:S(2)}) copy-start(f32[448,16,64]{0,1,2:T(8,128)} %get-tuple-element.69) | copy-start | bytes 5505028
  578.4 21.8 %collective-permute-start.1 = (f32[32]{0:T(128)S(1)}, f32[32]{0:T(128)S(1)}, u32[]{:S(2)}, u32[]{:S(2)}) collective-permute-start(f32[32]{0:T(128)S(1)} %add.156), channel_id=1, source_target_pairs={{0,2},{1,3},{2,0},{3,1},{4,6},{5,7},{6,4},{7,5},{8,10},{9,11},{10,... | collective-permute-start | bytes 392 | tf_op jit(solution)/shard_map/ppermute | solution.py:127
  598.7 40.9 %copy-start.12 = (f32[448,32]{0,1:T(8,128)S(1)}, f32[448,32]{0,1:T(8,128)}, u32[]{:S(2)}) copy-start(f32[448,32]{0,1:T(8,128)} %copy-done.11) | copy-start | bytes 172036
  598.7 40.9 %copy-start.14 = (f32[448,32]{0,1:T(8,128)S(1)}, f32[448,32]{0,1:T(8,128)}, u32[]{:S(2)}) copy-start(f32[448,32]{0,1:T(8,128)} %copy-done.13) | copy-start | bytes 172036
  598.7 40.9 %copy-start.16 = (f32[448,32]{0,1:T(8,128)S(1)}, f32[448,32]{0,1:T(8,128)}, u32[]{:S(2)}) copy-start(f32[448,32]{0,1:T(8,128)} %copy-done.15) | copy-start | bytes 172036
  598.7 40.9 %copy-start.18 = (f32[448,32]{0,1:T(8,128)S(1)}, f32[448,32]{0,1:T(8,128)}, u32[]{:S(2)}) copy-start(f32[448,32]{0,1:T(8,128)} %copy-done.17) | copy-start | bytes 172036
  600.3 41.0 %collective-permute-start.2 = (f32[32]{0:T(128)S(1)}, f32[32]{0:T(128)S(1)}, u32[]{:S(2)}, u32[]{:S(2)}) collective-permute-start(f32[32]{0:T(128)S(1)} %add.157), channel_id=1, source_target_pairs={{0,4},{1,5},{2,6},{3,7},{4,0},{5,1},{6,2},{7,3},{8,12},{9,13},{10,... | collective-permute-start | bytes 392 | tf_op jit(solution)/shard_map/ppermute | solution.py:127
  641.2 6.5 collective-permute-start.3
  644.7 3.5 copy-start.1
